TPU v7x, 32 devices: a whole 2x2x4 slice. The times are simulated.
32 devices in a mesh: dp: 8 (over z, core), mp: 4 (over y, x).
Axes of the slice: x: 2, y: 2, z: 4, core: 2. Of those that a mesh axis runs over, the one named last changes fastest.
Arguments:
- block_input: bfloat16 [4096, 6144], P('dp', 'mp'), may hold values from -6 to 6
- prenorm_gain: float32 [6144], P('mp'), may hold values from 0.5 to 1.5
- weight: bfloat16 [6144, 3072], P('mp', 'dp'), may hold values from -0.078125 to 0.078125
- query: bfloat16 [4096, 3072], P('dp'), may hold values from -6 to 6
- grad_normed: bfloat16 [4096, 3072], P('dp'), may hold values from -6 to 6
- qk_gain: float32 [128], replicated, may hold values from 0.5 to 1.5
Outputs:
- input_gradient: bfloat16 [4096, 6144], P('dp', 'mp')
- grad_weight: float32 [6144, 3072], P('mp', 'dp')
- prenorm_gain_gradient: float32 [6144], P('mp')
- grad_qk_gain: float32 [128], replicated
All inputs are finite; a program needn't handle non-finite values.
Results may differ from a plain program's by a relative error of at most 0.0049.
Values may be sent and summed in bfloat16 or wider, within the bound.
A program may use at most 128 MiB of HBM per device.

v0:
```python
import jax
import jax.numpy as jnp
from jax import lax
from jax.sharding import PartitionSpec as P

D = 6144


EPS = 1e-06


def qk_block(query, grad_normed, qk_gain):
    row_count = query.shape[0]
    head_size = qk_gain.shape[0]
    head_count = query.shape[1] // head_size
    q_float = query.astype(jnp.float32).reshape(row_count, head_count, head_size)
    q_mean = jnp.mean(q_float, axis=2, keepdims=True)
    q_var = jnp.mean(q_float * q_float, axis=2, keepdims=True) - q_mean * q_mean
    q_inv = lax.rsqrt(q_var + EPS)
    qhat = (q_float - q_mean) * q_inv
    upstream = grad_normed.astype(jnp.float32).reshape(row_count, head_count, head_size)
    dqhat = upstream * qk_gain
    grad_query = q_inv * (
        dqhat
        - jnp.mean(dqhat, axis=2, keepdims=True)
        - qhat * jnp.mean(dqhat * qhat, axis=2, keepdims=True)
    )
    contrib = jnp.sum(upstream * qhat, axis=1)
    return (grad_query.reshape(row_count, -1).astype(jnp.bfloat16), contrib)


def qk_backward(query, grad_normed, qk_gain):
    row_count = query.shape[0]
    block_rows = 128
    block_count = row_count // block_rows
    width_all = query.shape[1]
    query_blocks = query.reshape(block_count, block_rows, width_all)
    grad_blocks = grad_normed.reshape(block_count, block_rows, width_all)
    grad_query, contrib = lax.map(
        lambda pair: qk_block(pair[0], pair[1], qk_gain), (query_blocks, grad_blocks)
    )
    return (grad_query.reshape(row_count, width_all), contrib.reshape(row_count, -1))


def shards(block_input, prenorm_gain, weight, query, grad_normed, qk_gain):
    row_count = block_input.shape[0]
    input_wide_float = block_input.astype(jnp.float32)
    local_sum = jnp.sum(input_wide_float, axis=1)
    local_square = jnp.sum(input_wide_float * input_wide_float, axis=1)
    share_rows = row_count // lax.axis_size("mp")
    first_row = lax.axis_index("mp") * share_rows
    grad_query, contrib = qk_backward(query, grad_normed, qk_gain)
    qk_partial = jnp.sum(lax.dynamic_slice_in_dim(contrib, first_row, share_rows, 0), axis=0)
    gradient_prenormed_input = lax.dot_general(
        grad_query,
        lax.all_gather(weight, "dp", axis=1, tiled=True),
        (((1,), (1,)), ((), ())),
        preferred_element_type=jnp.float32,
    )
    standardized_gradient = gradient_prenormed_input * prenorm_gain
    total_sum, total_square, qk_mp = lax.psum((local_sum, local_square, qk_partial), "mp")
    row_average = (total_sum / D)[:, None]
    reciprocal_deviation = lax.rsqrt((total_square / D)[:, None] - row_average * row_average + EPS)
    standardized_input = (input_wide_float - row_average) * reciprocal_deviation
    slope_mean, slope_cross = lax.psum(
        (
            jnp.sum(standardized_gradient, axis=1),
            jnp.sum(standardized_gradient * standardized_input, axis=1),
        ),
        "mp",
    )
    average_standardized_gradient = (slope_mean / D)[:, None]
    average_cross_term = (slope_cross / D)[:, None]
    prenormed_rows = (standardized_input * prenorm_gain).astype(jnp.bfloat16)
    input_gradient = (
        reciprocal_deviation
        * (
            standardized_gradient
            - average_standardized_gradient
            - standardized_input * average_cross_term
        )
    ).astype(jnp.bfloat16)
    prenorm_gain_partial = jnp.sum(gradient_prenormed_input * standardized_input, axis=0)
    weight_partial = lax.dot_general(
        prenormed_rows, grad_query, (((0,), (0,)), ((), ())), preferred_element_type=jnp.float32
    )
    grad_weight = lax.psum_scatter(weight_partial, "dp", scatter_dimension=1, tiled=True)
    prenorm_gain_gradient, grad_qk_gain = lax.psum((prenorm_gain_partial, qk_mp), "dp")
    return (input_gradient, grad_weight, prenorm_gain_gradient, grad_qk_gain)


def solution(mesh):
    return jax.shard_map(
        shards,
        mesh=mesh,
        in_specs=(P("dp", "mp"), P("mp"), P("mp", "dp"), P("dp", None), P("dp", None), P()),
        out_specs=(P("dp", "mp"), P("mp", "dp"), P("mp"), P()),
        check_vma=False,
    )
```

profile of v0, /device:TPU:0, one launch (start us, length us, event | category | flops | bytes accessed | tf_op | source)
XLA Modules:
  0.0 319.4 jit_solution(11885546317323771219)
XLA Ops:
  8.0 1.9 fusion.7
  9.9 11.4 %all-reduce.2 = (f32[512]{0:T(512)S(1)}, f32[512]{0:T(512)S(1)}) all-reduce(f32[512]{0:T(512)S(1)} %get-tuple-element.48, f32[512]{0:T(512)S(1)} %get-tuple-element.47), channel_id=1, replica_groups=mesh['dp'=8,'mp'=4] {'mp'}, use_global_device_ids=true, to_apply=%region_3.0 | all-reduce | flops 1024 | bytes 8192 | tf_op jit(solution)/shard_map/psum | solution.py:61
  21.3 91.3 %while.12 = (s32[]{:T(128)}, bf16[4,128,3072]{2,1,0:T(8,128)(2,1)}, f32[4,128,128]{2,1,0:T(8,128)}, bf16[4,128,3072]{2,1,0:T(8,128)(2,1)}, bf16[4,128,3072]{2,1,0:T(8,128)(2,1)}, /*index=5*/f32[128]{0:T(128)}, s32[]{:T(128)}) while((s32[]{:T(128)}, bf16[4,128,3072]{2,1,0:T(8,128)(2,1)}, f32[4,128,128]{2,1,0:T(8,128)}, ...), condition=%wide.region_10.11_spmd, body=%wide.region_4.10_spmd.sunk | while | flops 9823234 | bytes 46845052 | solution.py:39
  22.0 1.7 convert_bitcast_fusion.3
  25.2 2.2 multiply_reduce_fusion.6
  28.8 1.6 mul.293
  31.9 1.6 sub.158
  33.5 2.6 sub.159
  37.7 2.6 mul.292
  40.3 3.9 %fusion.31 = bf16[4,128,3072]{2,1,0:T(8,128)(2,1)} fusion(bf16[4,128,3072]{2,1,0:T(8,128)(2,1)} %get-tuple-element.140, s32[]{:T(128)S(6)} %copy.21, f32[1,128,3072]{2,1,0:T(8,128)} %mul.292, f32[1,128,3072]{2,1,0:T(8,128)S(1)} %mul.294, f32[1,128,3072]{2,1,0:T(8,128)} %sub.159, f32[1,128,3072]{2,1,0:T(8,128)S(1)} %sub.161, ...), kind=kLoop, calls=%fused_computation.15.clone.1 | loop fusion | flops 3932160 | bytes 8663044 | tf_op jit(solution)/shard_map/while/body/jit(dynamic_update_index_in_dim)/dynamic_update_slice | solution.py:39
  48.0 2.2 multiply_reduce_fusion.6
  51.5 1.6 mul.293
  54.7 1.6 sub.158
  56.3 2.6 sub.159
  60.5 2.6 mul.292
  63.0 4.0 %fusion.31 = bf16[4,128,3072]{2,1,0:T(8,128)(2,1)} fusion(bf16[4,128,3072]{2,1,0:T(8,128)(2,1)} %get-tuple-element.140, s32[]{:T(128)S(6)} %copy.21, f32[1,128,3072]{2,1,0:T(8,128)} %mul.292, f32[1,128,3072]{2,1,0:T(8,128)S(1)} %mul.294, f32[1,128,3072]{2,1,0:T(8,128)} %sub.159, f32[1,128,3072]{2,1,0:T(8,128)S(1)} %sub.161, ...), kind=kLoop, calls=%fused_computation.15.clone.1 | loop fusion | flops 3932160 | bytes 8663044 | tf_op jit(solution)/shard_map/while/body/jit(dynamic_update_index_in_dim)/dynamic_update_slice | solution.py:39
  70.8 2.2 multiply_reduce_fusion.6
  77.5 1.6 sub.158
  79.1 2.6 sub.159
  83.3 2.5 mul.292
  85.9 4.0 %fusion.31 = bf16[4,128,3072]{2,1,0:T(8,128)(2,1)} fusion(bf16[4,128,3072]{2,1,0:T(8,128)(2,1)} %get-tuple-element.140, s32[]{:T(128)S(6)} %copy.21, f32[1,128,3072]{2,1,0:T(8,128)} %mul.292, f32[1,128,3072]{2,1,0:T(8,128)S(1)} %mul.294, f32[1,128,3072]{2,1,0:T(8,128)} %sub.159, f32[1,128,3072]{2,1,0:T(8,128)S(1)} %sub.161, ...), kind=kLoop, calls=%fused_computation.15.clone.1 | loop fusion | flops 3932160 | bytes 8663044 | tf_op jit(solution)/shard_map/while/body/jit(dynamic_update_index_in_dim)/dynamic_update_slice | solution.py:39
  93.6 2.2 multiply_reduce_fusion.6
  100.3 1.6 sub.158
  101.9 2.6 sub.159
  106.1 2.5 mul.292
  108.6 3.9 %fusion.31 = bf16[4,128,3072]{2,1,0:T(8,128)(2,1)} fusion(bf16[4,128,3072]{2,1,0:T(8,128)(2,1)} %get-tuple-element.140, s32[]{:T(128)S(6)} %copy.21, f32[1,128,3072]{2,1,0:T(8,128)} %mul.292, f32[1,128,3072]{2,1,0:T(8,128)S(1)} %mul.294, f32[1,128,3072]{2,1,0:T(8,128)} %sub.159, f32[1,128,3072]{2,1,0:T(8,128)S(1)} %sub.161, ...), kind=kLoop, calls=%fused_computation.15.clone.1 | loop fusion | flops 3932160 | bytes 8663044 | tf_op jit(solution)/shard_map/while/body/jit(dynamic_update_index_in_dim)/dynamic_update_slice | solution.py:39
  112.6 11.4 %fusion.19 = f32[1536,3072]{1,0:T(8,128)} fusion(bf16[512,3072]{1,0:T(8,128)(2,1)} %bitcast.36, bf16[512,1536]{1,0:T(8,128)(2,1)} %param.8, f32[512]{0:T(512)S(1)} %get-tuple-element.73, f32[1536]{0:T(1024)S(1)} %copy-done.2, f32[512]{0:T(512)S(1)} %get-tuple-element.72), kind=kOutput, calls=%fused_computation.38 | convolution fusion | flops 4835770368 | bytes 23603200 | tf_op jit(solution)/shard_map/dot_general | solution.py:84
  125.4 11.2 %fusion.18 = (f32[1536]{0:T(1024)S(1)}, f32[512]{0:T(512)S(1)}, f32[512]{0:T(512)S(1)}, f32[512,1536]{1,0:T(8,128)}) fusion(bf16[512,1536]{1,0:T(8,128)(2,1)S(1)} %copy-done, f32[512]{0:T(512)S(1)} %get-tuple-element.73, f32[512]{0:T(512)S(1)} %get-tuple-element.72, f32[1536]{0:T(1024)S(1)} %copy-done.2, bf16[512,3072]{1,0:T(8,128)(2,1)} %bitcast.37, ...), kind=kOutput, calls=%fused_computation.36 | convolution fusion | flops 4838913536 | bytes 17321984 | tf_op jit(solution)/shard_map/dot_general | solution.py:54
  136.6 8.4 %all-reduce.1 = (f32[512]{0:T(512)S(1)}, f32[512]{0:T(512)S(1)}, f32[128]{0:T(128)S(1)}) all-reduce(f32[512]{0:T(512)S(1)} %get-tuple-element.45, f32[512]{0:T(512)S(1)} %get-tuple-element.46, f32[128]{0:T(128)S(1)} %dynamic-slice_reduce_fusion), channel_id=1, replica_groups=mesh['dp'=8,'mp'=4] {'mp'}, use_global_device_ids=true, to_apply=%region_14.15 | all-reduce | flops 1152 | bytes 9216 | tf_op jit(solution)/shard_map/psum | solution.py:65
  145.1 16.2 %all-reduce = (f32[1536]{0:T(1024)}, f32[128]{0:T(128)}) all-reduce(f32[1536]{0:T(1024)S(1)} %get-tuple-element.44, f32[128]{0:T(128)S(1)} %get-tuple-element.65), channel_id=1, replica_groups=mesh['dp'=8,'mp'=4] {'dp'}, use_global_device_ids=true, to_apply=%region_17.18 | all-reduce | flops 1664 | bytes 13312 | tf_op jit(solution)/shard_map/psum | solution.py:88
  161.2 4.0 %fusion.16 = bf16[512,1536]{1,0:T(8,128)(2,1)} fusion(bf16[512,1536]{1,0:T(8,128)(2,1)S(1)} %copy-done, f32[512,1536]{1,0:T(8,128)} %get-tuple-element.74, f32[512]{0:T(512)S(1)} %get-tuple-element.75, f32[512]{0:T(512)S(1)} %get-tuple-element.73, f32[512]{0:T(512)S(1)} %get-tuple-element.76, f32[1536]{0:T(1024)S(1)} %copy-done.2, f32[512]{0:T(512)S(1)} %get-tuple-element.72), kind=kLoop, calls=%fused_computation.34 | loop fusion | flops 7077888 | bytes 6305792 | tf_op jit(solution)/shard_map/convert_element_type | solution.py:82
  165.2 147.3 %reduce-scatter.2.cloned.1.call-done = f32[1536,384]{1,0:T(8,128)} async-done(((f32[1536,3072]{1,0:T(8,128)}), f32[1536,384]{1,0:T(8,128)}) %reduce-scatter.2.cloned.1.call-update) | async-done | bytes 2359312 | tf_op jit(solution)/shard_map/reduce_scatter | solution.py:87
  (75 shorter events, 36.7 us)
Async XLA Ops:
  7.2 117.9 %all-gather.2.cloned.1.call-start = ((), (), s32[]{:S(2)}) async-start(), calls=%async_computation.1 | async-start | bytes 10616832 | tf_op jit(solution)/shard_map/all_gather | solution.py:56
  7.9 304.6 %reduce-scatter.2.cloned.1.call-start = ((), (), s32[]{:S(2)}) async-start(), calls=%async_computation.2 | async-start | bytes 21233664 | tf_op jit(solution)/shard_map/reduce_scatter | solution.py:87
  21.3 91.3 %copy-start.2 = (f32[1536]{0:T(1024)S(1)}, f32[1536]{0:T(1024)}, u32[]{:S(2)}) copy-start(f32[1536]{0:T(1024)} %param.9) | copy-start | bytes 18436
  24.0 1.2 copy-start.1
  46.8 1.2 copy-start.1
  69.6 1.2 copy-start.1
  92.4 1.2 copy-start.1
  124.0 1.4 copy-start
Sparse Core Ops, SparseCore 0:
  9.6 93.3 all-gather.1
  124.1 188.3 reduce-scatter.1
where the time goes:
time: 320 us; the launch traced here: 319 us
  waiting for transfers between devices  148 us (46%)
  local copies, waits for them, and re-layouts  56.6 us (18%)
  other arithmetic  41.6 us (13%)
  blocking collectives  36 us (11%)
  matrix products  22.6 us (7%)
  between operations  14.1 us (4%)
    reduce_scatter x1, waiting for transfers between devices, shards(): lax.psum_scatter(weight_partial, 'dp', scatter_dimension=1, tiled=True)  147 us
    sub x8, local copies, waits for them, and re-layouts, qk_block(): qhat = (q_float - q_mean) * q_inv  16.8 us
    mul x8, local copies, waits for them, and re-layouts, qk_block(): q_inv * (dqhat - jnp.mean(dqhat, axis=2, keepdims=True) - qhat * jnp.mean...  16.6 us
    psum x1, blocking collectives, shards(): lax.psum((prenorm_gain_partial, qk_mp), 'dp')  16.2 us
    dynamic_update_slice x4, other arithmetic, qk_backward(): lax.map(lambda pair: qk_block(pair[0], pair[1], qk_gain), (query_blocks,...  15.9 us
    mul x8, local copies, waits for them, and re-layouts, qk_block(): qhat * jnp.mean(dqhat * qhat, axis=2, keepdims=True)  12.6 us
    dot_general x1, matrix products, shards(): lax.dot_general(prenormed_rows, grad_query, (((0,), (0,)), ((), ())), pre...  11.4 us
    psum x1, blocking collectives, shards(): lax.psum((local_sum, local_square, qk_partial), 'mp')  11.4 us
  transfers between devices with their start and end apart: 2, of which 1 were waited for; matrix products, arithmetic and copies ran while one was open for 38% of the time, Pallas kernels for 0%

commit v1 on v0

v1 whole, which is shorter than its diff:
```python
import jax
import jax.numpy as jnp
from jax import lax
from jax.experimental import pallas as pl
from jax.experimental.pallas import tpu as pltpu
from jax.sharding import PartitionSpec as P

D = 6144


EPS = 1e-06


def qk_kernel(query_ref, grad_ref, gain_ref, out_ref, contrib_ref):
    @pl.when(pl.program_id(0) == 0)
    def _():
        contrib_ref[...] = jnp.zeros_like(contrib_ref)

    head_size = gain_ref.shape[1]
    gain = gain_ref[...]
    total = jnp.zeros_like(contrib_ref)
    for head in range(query_ref.shape[1] // head_size):
        columns = pl.ds(head * head_size, head_size)
        q_float = query_ref[:, columns].astype(jnp.float32)
        upstream = grad_ref[:, columns].astype(jnp.float32)
        q_mean = jnp.mean(q_float, axis=1, keepdims=True)
        q_var = jnp.mean(q_float * q_float, axis=1, keepdims=True) - q_mean * q_mean
        q_inv = lax.rsqrt(q_var + EPS)
        qhat = (q_float - q_mean) * q_inv
        dqhat = upstream * gain
        dq_mean = jnp.mean(dqhat, axis=1, keepdims=True)
        dq_cross = jnp.mean(dqhat * qhat, axis=1, keepdims=True)
        out_ref[:, columns] = (q_inv * (dqhat - dq_mean - qhat * dq_cross)).astype(out_ref.dtype)
        product = upstream * qhat
        total += jnp.sum(product.reshape(-1, 8, head_size), axis=0)
    contrib_ref[...] += total


def qk_backward(query, grad_normed, qk_gain):
    rows, width = query.shape
    head_size = qk_gain.shape[0]
    block = min(rows, 64)
    grad_query, contrib = pl.pallas_call(
        qk_kernel,
        grid=(rows // block,),
        in_specs=[
            pl.BlockSpec((block, width), lambda i: (i, 0)),
            pl.BlockSpec((block, width), lambda i: (i, 0)),
            pl.BlockSpec((1, head_size), lambda i: (0, 0)),
        ],
        out_specs=[
            pl.BlockSpec((block, width), lambda i: (i, 0)),
            pl.BlockSpec((8, head_size), lambda i: (0, 0)),
        ],
        out_shape=[
            jax.ShapeDtypeStruct((rows, width), jnp.bfloat16),
            jax.ShapeDtypeStruct((8, head_size), jnp.float32),
        ],
        compiler_params=pltpu.CompilerParams(vmem_limit_bytes=32 * 1024 * 1024),
        cost_estimate=pl.CostEstimate(flops=40 * rows * width, bytes_accessed=6 * rows * width, transcendentals=0),
    )(query, grad_normed, qk_gain.reshape(1, -1))
    return grad_query, jnp.sum(contrib, axis=0)


def shards(block_input, prenorm_gain, weight, query, grad_normed, qk_gain):
    input_wide_float = block_input.astype(jnp.float32)
    local_sum = jnp.sum(input_wide_float, axis=1)
    local_square = jnp.sum(input_wide_float * input_wide_float, axis=1)
    grad_query, qk_partial = qk_backward(query, grad_normed, qk_gain)
    gradient_prenormed_input = lax.dot_general(
        grad_query,
        lax.all_gather(weight, "dp", axis=1, tiled=True),
        (((1,), (1,)), ((), ())),
        preferred_element_type=jnp.float32,
    )
    standardized_gradient = gradient_prenormed_input * prenorm_gain
    total_sum, total_square = lax.psum((local_sum, local_square), "mp")
    row_average = (total_sum / D)[:, None]
    reciprocal_deviation = lax.rsqrt((total_square / D)[:, None] - row_average * row_average + EPS)
    standardized_input = (input_wide_float - row_average) * reciprocal_deviation
    slope_mean, slope_cross = lax.psum(
        (
            jnp.sum(standardized_gradient, axis=1),
            jnp.sum(standardized_gradient * standardized_input, axis=1),
        ),
        "mp",
    )
    average_standardized_gradient = (slope_mean / D)[:, None]
    average_cross_term = (slope_cross / D)[:, None]
    prenormed_rows = (standardized_input * prenorm_gain).astype(jnp.bfloat16)
    input_gradient = (
        reciprocal_deviation
        * (
            standardized_gradient
            - average_standardized_gradient
            - standardized_input * average_cross_term
        )
    ).astype(jnp.bfloat16)
    prenorm_gain_partial = jnp.sum(gradient_prenormed_input * standardized_input, axis=0)
    weight_partial = lax.dot_general(
        prenormed_rows, grad_query, (((0,), (0,)), ((), ())), preferred_element_type=jnp.float32
    )
    grad_weight = lax.psum_scatter(
        weight_partial.astype(jnp.bfloat16), "dp", scatter_dimension=1, tiled=True
    ).astype(jnp.float32)
    prenorm_gain_gradient, grad_qk_gain = lax.psum((prenorm_gain_partial, qk_partial), "dp")
    return (input_gradient, grad_weight, prenorm_gain_gradient, grad_qk_gain)


def solution(mesh):
    return jax.shard_map(
        shards,
        mesh=mesh,
        in_specs=(P("dp", "mp"), P("mp"), P("mp", "dp"), P("dp", None), P("dp", None), P()),
        out_specs=(P("dp", "mp"), P("mp", "dp"), P("mp"), P()),
        check_vma=False,
    )
```

time: 320 us -> 215 us (0.67)
  waiting for transfers between devices: 148 us -> 98.1 us
  local copies, waits for them, and re-layouts: 56.6 us -> 19.5 us
  other arithmetic: 41.6 us -> 8.08 us
  Pallas kernels: 0 us -> 18.1 us
  matrix products: 22.6 us -> 19 us
    reduce_scatter x1 -> x0, waiting for transfers between devices: 147 us -> none  [shards(): lax.psum_scatter(weight_partial, 'dp', scatter_dimension=1, tiled=True)]
    unnamed x2 -> x3, waiting for transfers between devices: 0.7 us -> 60.4 us
    all_gather x1, waiting for transfers between devices: 0.01 us -> 37.7 us  [shards(): lax.all_gather(weight, 'dp', axis=1, tiled=True)]
    mul x20 -> x0, local copies, waits for them, and re-layouts: 31.9 us -> none  [the longest x8 16.6 us: qk_block(): q_inv * (dqhat - jnp.mean(dqhat, axis=2, keepdims=True) - qhat * jnp.mean...]
    sub x16 -> x0, local copies, waits for them, and re-layouts: 19.6 us -> none  [the longest x8 16.8 us: qk_block(): qhat = (q_float - q_mean) * q_inv]
    unnamed x4 -> x12, local copies, waits for them, and re-layouts: 0.41 us -> 19.5 us
    pallas_call x0 -> x1, Pallas kernels: none -> 18.1 us  [qk_backward(): pl.pallas_call(qk_kernel, grid=(rows // block,), in_specs=[pl.BlockSpec((...]
    dynamic_update_slice x4 -> x0, other arithmetic: 15.9 us -> none  [qk_backward(): lax.map(lambda pair: qk_block(pair[0], pair[1], qk_gain), (query_blocks,...]
  transfers between devices with their start and end apart: 2 -> 2, of which waited for: 1 -> 2; matrix products, arithmetic and copies ran while one was open for 38% -> 18% of each run, Pallas kernels for 0% -> 8%
where the time goes in v1:
time: 215 us; the launch traced here: 214 us
  waiting for transfers between devices  98.1 us (46%)
  blocking collectives  37.3 us (17%)
  local copies, waits for them, and re-layouts  19.5 us (9%)
  matrix products  19 us (9%)
  Pallas kernels  18.1 us (8%)
  between operations  14.1 us (7%)
  other arithmetic  8.08 us (4%)
    unnamed x3, waiting for transfers between devices  60.4 us
    all_gather x1, waiting for transfers between devices, shards(): lax.all_gather(weight, 'dp', axis=1, tiled=True)  37.7 us
    unnamed x12, local copies, waits for them, and re-layouts  19.5 us
    pallas_call x1, Pallas kernels, qk_backward(): pl.pallas_call(qk_kernel, grid=(rows // block,), in_specs=[pl.BlockSpec((...  18.1 us
    psum x1, blocking collectives, shards(): lax.psum((prenorm_gain_partial, qk_partial), 'dp')  16.1 us
    psum x1, blocking collectives, shards(): total_sum, total_square = lax.psum((local_sum, local_square), 'mp')  11.4 us
    dot_general x1, matrix products, shards(): lax.dot_general(grad_query, lax.all_gather(weight, 'dp', axis=1, tiled=Tr...  11 us
    psum x1, blocking collectives, shards(): lax.psum((jnp.sum(standardized_gradient, axis=1), jnp.sum(standardized_gr...  9.81 us
  transfers between devices with their start and end apart: 2, of which 2 were waited for; matrix products, arithmetic and copies ran while one was open for 18% of the time, Pallas kernels for 8%

profile of v1, /device:TPU:0, one launch (start us, length us, event | category | flops | bytes accessed | tf_op | source)
XLA Modules:
  0.0 214.2 jit_solution(13989482667517866858)
XLA Ops:
  7.2 0.0 all-gather.2.cloned.1.call-start
  7.2 0.7 all-gather.2.cloned.1.call-update
  7.9 0.0 reduce-scatter.4.cloned.1.call-start
  7.9 1.9 fusion
  9.9 11.4 %all-reduce.2 = (f32[512]{0:T(512)S(1)}, f32[512]{0:T(512)S(1)}) all-reduce(f32[512]{0:T(512)S(1)} %get-tuple-element.12, f32[512]{0:T(512)S(1)} %get-tuple-element.11), channel_id=1, replica_groups=mesh['dp'=8,'mp'=4] {'mp'}, use_global_device_ids=true, to_apply=%region_3.0 | all-reduce | flops 1024 | bytes 8192 | tf_op jit(solution)/shard_map/psum | solution.py:77
  21.3 0.0 copy-start
  21.3 2.5 %copy-done = bf16[512,3072]{1,0:T(8,128)(2,1)S(1)} copy-done((bf16[512,3072]{1,0:T(8,128)(2,1)S(1)}, bf16[512,3072]{1,0:T(8,128)(2,1)}, u32[]{:S(2)}) %copy-start) | copy-done | bytes 3145752
  23.8 0.0 copy-start.1
  23.8 1.9 copy-done.1
  25.7 0.0 copy-start.2
  25.7 0.7 copy-done.2
  26.3 0.0 copy-start.3
  26.3 0.0 copy-start.4
  26.3 18.1 %shard_map.93 = (bf16[512,3072]{1,0:T(8,128)(2,1)S(1)}, f32[8,128]{1,0:T(8,128)S(1)}) custom-call(bf16[512,3072]{1,0:T(8,128)(2,1)S(1)} %copy-done, bf16[512,3072]{1,0:T(8,128)(2,1)S(1)} %copy-done.1, f32[1,128]{1,0:T(1,128)S(1)} %bitcast.6), custom_call_target="tpu_custom_call" | custom-call | flops 62914560 | bytes 9437184 | tf_op jit(solution)/shard_map/pallas_call | solution.py:43
  44.5 0.0 copy-done.3
  44.5 0.0 copy-done.4
  44.5 7.9 %convolution_convert_fusion = bf16[1536,3072]{1,0:T(8,128)(2,1)} fusion(bf16[512,3072]{1,0:T(8,128)(2,1)S(1)} %get-tuple-element.6, bf16[512,1536]{1,0:T(8,128)(2,1)S(1)} %copy-done.3, f32[512]{0:T(512)S(1)} %get-tuple-element.20, f32[1536]{0:T(1024)S(1)} %copy-done.4, f32[512]{0:T(512)S(1)} %get-tuple-element.19), kind=kOutput, calls=%fused_computation | convolution fusion | flops 4840488960 | bytes 14166016 | tf_op jit(solution)/shard_map/dot_general | solution.py:100
  52.4 12.7 %copy.10 = bf16[1536,3072]{0,1:T(8,128)(2,1)} copy(bf16[1536,3072]{1,0:T(8,128)(2,1)} %convolution_convert_fusion) | data formatting | bytes 18874368
  65.2 0.0 reduce-scatter.4.cloned.1.call-update
  65.2 37.7 %all-gather.2.cloned.1.call-done = bf16[1536,3072]{1,0:T(8,128)(2,1)} async-done(((bf16[1536,384]{1,0:T(8,128)(2,1)}), bf16[1536,3072]{1,0:T(8,128)(2,1)}) %all-gather.2.cloned.1.call-update) | async-done | bytes 9437200 | tf_op jit(solution)/shard_map/all_gather | solution.py:72
  102.9 11.0 %fusion.11 = (f32[1536]{0:T(1024)S(1)}, f32[512]{0:T(512)S(1)}, f32[512]{0:T(512)S(1)}, f32[512,1536]{1,0:T(8,128)}) fusion(bf16[512,1536]{1,0:T(8,128)(2,1)} %param.6, f32[512]{0:T(512)S(1)} %get-tuple-element.20, f32[512]{0:T(512)S(1)} %get-tuple-element.19, f32[1536]{0:T(1024)S(1)} %copy-done.4, bf16[512,3072]{1,0:T(8,128)(2,1)S(1)} %get-tuple-element.6, ...), kind=kOutput, calls=%fused_computation.15 | convolution fusion | flops 4838913536 | bytes 17321984 | tf_op jit(solution)/shard_map/dot_general | solution.py:70
  114.0 9.8 %all-reduce.1 = (f32[512]{0:T(512)S(1)}, f32[512]{0:T(512)S(1)}) all-reduce(f32[512]{0:T(512)S(1)} %get-tuple-element.9, f32[512]{0:T(512)S(1)} %get-tuple-element.10), channel_id=1, replica_groups=mesh['dp'=8,'mp'=4] {'mp'}, use_global_device_ids=true, to_apply=%region_7.0 | all-reduce | flops 1024 | bytes 8192 | tf_op jit(solution)/shard_map/psum | solution.py:81
  123.8 16.1 %all-reduce = (f32[1536]{0:T(1024)}, f32[128]{0:T(128)}) all-reduce(f32[1536]{0:T(1024)S(1)} %get-tuple-element.8, f32[128]{0:T(128)S(1)} %reduce_sum.59), channel_id=1, replica_groups=mesh['dp'=8,'mp'=4] {'dp'}, use_global_device_ids=true, to_apply=%region_10.0 | all-reduce | flops 1664 | bytes 13312 | tf_op jit(solution)/shard_map/psum | solution.py:106
  139.9 4.6 %fusion.9 = bf16[512,1536]{1,0:T(8,128)(2,1)} fusion(bf16[512,1536]{1,0:T(8,128)(2,1)} %param.6, f32[512,1536]{1,0:T(8,128)} %get-tuple-element.21, f32[512]{0:T(512)S(1)} %get-tuple-element.22, f32[512]{0:T(512)S(1)} %get-tuple-element.20, f32[512]{0:T(512)S(1)} %get-tuple-element.23, f32[1536]{0:T(1024)S(1)} %copy-done.4, f32[512]{0:T(512)S(1)} %get-tuple-element.19), kind=kLoop, calls=%fused_computation.13 | loop fusion | flops 7077888 | bytes 6305792 | tf_op jit(solution)/shard_map/convert_element_type | solution.py:98
  144.4 59.7 %reduce-scatter.4.cloned.1.call-done = bf16[384,1536]{1,0:T(8,128)(2,1)} async-done(((bf16[3072,1536]{1,0:T(8,128)(2,1)}), bf16[384,1536]{1,0:T(8,128)(2,1)}) %reduce-scatter.4.cloned.1.call-update) | async-done | bytes 1179664
  204.1 1.7 copy.11
  205.8 1.6 convert_element_type.19
  (3 shorter events, 0.0 us)
Async XLA Ops:
  7.2 95.8 %all-gather.2.cloned.1.call-start = ((), (), s32[]{:S(2)}) async-start(), calls=%async_computation.1 | async-start | bytes 10616832 | tf_op jit(solution)/shard_map/all_gather | solution.py:72
  7.9 196.2 %reduce-scatter.4.cloned.1.call-start = ((), (), s32[]{:S(2)}) async-start(), calls=%async_computation.2 | async-start | bytes 10616832
  21.3 2.5 %copy-start = (bf16[512,3072]{1,0:T(8,128)(2,1)S(1)}, bf16[512,3072]{1,0:T(8,128)(2,1)}, u32[]{:S(2)}) copy-start(bf16[512,3072]{1,0:T(8,128)(2,1)} %query_ref.1) | copy-start | bytes 9437188
  23.8 1.9 copy-start.1
  25.7 0.7 copy-start.2
  26.3 18.2 %copy-start.3 = (bf16[512,1536]{1,0:T(8,128)(2,1)S(1)}, bf16[512,1536]{1,0:T(8,128)(2,1)}, u32[]{:S(2)}) copy-start(bf16[512,1536]{1,0:T(8,128)(2,1)} %param.6) | copy-start | bytes 4718596
  26.3 18.2 %copy-start.4 = (f32[1536]{0:T(1024)S(1)}, f32[1536]{0:T(1024)}, u32[]{:S(2)}) copy-start(f32[1536]{0:T(1024)} %param.7) | copy-start | bytes 18436
Sparse Core Ops, SparseCore 0:
  9.6 93.3 all-gather.1
  105.2 98.8 reduce-scatter.3
